TPU v7x, 32 devices: a whole 2x2x4 slice. The times are simulated.
32 devices in a mesh: shard: 16 (over z, y, core), model: 2 (over x).
Axes of the slice: x: 2, y: 2, z: 4, core: 2. Of those that a mesh axis runs over, the one named last changes fastest.
Arguments:
- gradients: float32 [128, 128, 4096], P(None, 'shard', 'model'), may hold values from -6 to 6
- momentum: float32 [128, 128, 4096], P(None, 'shard', 'model'), may hold values from -6 to 6
- weights: float32 [128, 128, 4096], P(None, 'shard', 'model'), may hold values from -0.1875 to 0.1875
Outputs:
- new_weights: float32 [128, 128, 4096], P(None, 'shard', 'model')
- new_momentum: float32 [128, 128, 4096], P(None, 'shard', 'model')
All inputs are finite; a program needn't handle non-finite values.
Results may differ from a plain program's by a relative error of at most 0.0001.
Values sent between devices are 32-bit elements; how exact they have to be, the bound alone decides.
A program may use at most 128 MiB of HBM per device.

v0:
```python
import jax
import jax.numpy as jnp
from jax import lax
from jax.sharding import PartitionSpec as P

ITERS = 3
hold_rate = 0.9
learn_rate = 0.9
decay_rate = 0.1


def body(gradients, momentum, weights):
    new_momentum = hold_rate * momentum + gradients
    moved = lax.all_to_all(new_momentum, "shard", split_axis=0, concat_axis=1, tiled=True)
    total = lax.psum(jnp.sum(moved * moved, axis=(1, 2), keepdims=True), "model")
    iterate = moved * lax.rsqrt(total + 1e-06)
    for step in range(ITERS):
        gram = lax.psum(
            jnp.einsum("mik,mjk->mij", iterate, iterate, precision=lax.Precision.HIGHEST), "model"
        )
        mixed = -4.775 * gram + 2.0315 * jnp.einsum(
            "mij,mjk->mik", gram, gram, precision=lax.Precision.HIGHEST
        )
        iterate = 3.4445 * iterate + jnp.einsum(
            "mij,mjk->mik", mixed, iterate, precision=lax.Precision.HIGHEST
        )
    back = lax.all_to_all(iterate, "shard", split_axis=1, concat_axis=0, tiled=True)
    new_weights = (1.0 - learn_rate * decay_rate) * weights - learn_rate * back
    return (new_weights, new_momentum)


def solution(mesh):
    placed = (P(None, "shard", "model"), P(None, "shard", "model"), P(None, "shard", "model"))
    return jax.shard_map(
        body,
        mesh=mesh,
        in_specs=placed,
        out_specs=(P(None, "shard", "model"), P(None, "shard", "model")),
        check_vma=False,
    )
```

profile of v0, /device:TPU:1, one launch (start us, length us, event | category | flops | bytes accessed | tf_op | source)
XLA Modules:
  0.0 612.2 jit_solution(11765519909520166831)
XLA Ops:
  7.2 12.0 %multiply_add_fusion.3 = f32[128,8,2048]{2,1,0:T(8,128)} fusion(f32[128,8,2048]{2,1,0:T(8,128)} %param.3, f32[128,8,2048]{2,1,0:T(8,128)} %param.4), kind=kLoop, calls=%fused_computation.7 | loop fusion | flops 4194304 | bytes 25165824 | tf_op jit(solution)/shard_map/add | solution.py:13
  19.2 189.9 %all_to_all.27 = f32[128,8,2048]{2,1,0:T(8,128)S(1)} all-to-all(f32[128,8,2048]{2,1,0:T(8,128)} %multiply_add_fusion.3), channel_id=1, replica_groups=mesh['shard'=16,'model'=2] {'shard'}, dimensions={0} | all-to-all | bytes 16777216 | tf_op jit(solution)/shard_map/all_to_all | solution.py:14
  209.1 3.4 copy-done
  212.5 0.8 fusion
  213.3 4.1 psum.28
  217.3 12.9 %fusion.2 = f32[8,128,128]{2,1,0:T(8,128)} fusion(f32[16,8,8,2048]{3,2,1,0:T(8,128)} %bitcast.38, f32[8]{0:T(128)S(1)} %rsqrt_bitcast_fusion), kind=kOutput, calls=%fused_computation.9 | convolution fusion | flops 3223322624 | bytes 8912928 | tf_op jit(solution)/shard_map/mik,mjk->mij/dot_general | solution.py:19
  230.8 28.8 %all-reduce.4.cloned.1.call-done = f32[8,128,128]{2,1,0:T(8,128)} async-done(((f32[8,128,128]{2,1,0:T(8,128)}), f32[8,128,128]{2,1,0:T(8,128)}) %all-reduce.4.cloned.1.call-update) | async-done | bytes 524304 | tf_op jit(solution)/shard_map/psum | solution.py:18
  259.6 2.1 fusion.7
  261.7 11.7 %multiply_add_fusion.2 = f32[8,128,2048]{2,1,0:T(8,128)S(1)} fusion(f32[16,8,8,2048]{3,2,1,0:T(8,128)} %bitcast.39, f32[8,128,128]{2,1,0:T(8,128)S(1)} %fusion.7, f32[8]{0:T(128)S(1)} %rsqrt_bitcast_fusion), kind=kOutput, calls=%fused_computation.6 | convolution fusion | flops 3229614080 | bytes 17301536 | tf_op jit(solution)/shard_map/mij,mjk->mik/dot_general | solution.py:24
  273.4 3.4 copy-done.1
  276.8 8.5 %fusion.8 = f32[8,128,128]{2,1,0:T(8,128)} fusion(f32[8,128,2048]{2,1,0:T(8,128)S(1)} %multiply_add_fusion.2), kind=kOutput, calls=%fused_computation.20 | convolution fusion | flops 3221225472 | bytes 8912896 | tf_op jit(solution)/shard_map/mik,mjk->mij/dot_general | solution.py:19
  285.4 28.8 %all-reduce.6.cloned.1.call-done = f32[8,128,128]{2,1,0:T(8,128)} async-done(((f32[8,128,128]{2,1,0:T(8,128)}), f32[8,128,128]{2,1,0:T(8,128)}) %all-reduce.6.cloned.1.call-update) | async-done | bytes 524304 | tf_op jit(solution)/shard_map/psum | solution.py:18
  314.1 2.1 fusion.6
  316.2 14.1 %multiply_add_fusion.1 = f32[8,128,2048]{2,1,0:T(8,128)S(1)} fusion(f32[8,128,2048]{2,1,0:T(8,128)} %copy-done.1, f32[8,128,128]{2,1,0:T(8,128)S(1)} %fusion.6), kind=kOutput, calls=%fused_computation.5 | convolution fusion | flops 3225419776 | bytes 17301504 | tf_op jit(solution)/shard_map/mij,mjk->mik/dot_general | solution.py:24
  330.3 3.4 copy-done.2
  333.7 8.5 %fusion.9 = f32[8,128,128]{2,1,0:T(8,128)} fusion(f32[8,128,2048]{2,1,0:T(8,128)S(1)} %multiply_add_fusion.1), kind=kOutput, calls=%fused_computation.21 | convolution fusion | flops 3221225472 | bytes 8912896 | tf_op jit(solution)/shard_map/mik,mjk->mij/dot_general | solution.py:19
  342.3 28.8 %all-reduce.8.cloned.1.call-done = f32[8,128,128]{2,1,0:T(8,128)} async-done(((f32[8,128,128]{2,1,0:T(8,128)}), f32[8,128,128]{2,1,0:T(8,128)}) %all-reduce.8.cloned.1.call-update) | async-done | bytes 524304 | tf_op jit(solution)/shard_map/psum | solution.py:18
  371.1 2.1 fusion.5
  373.2 15.0 %multiply_add_fusion = f32[8,128,2048]{2,1,0:T(8,128)S(1)} fusion(f32[8,128,2048]{2,1,0:T(8,128)} %copy-done.2, f32[8,128,128]{2,1,0:T(8,128)S(1)} %fusion.5), kind=kOutput, calls=%fused_computation.4 | convolution fusion | flops 3225419776 | bytes 17301504 | tf_op jit(solution)/shard_map/mij,mjk->mik/dot_general | solution.py:24
  388.2 4.9 copy.8
  393.1 188.9 %all_to_all.28 = f32[8,128,2048]{2,0,1:T(8,128)S(1)} all-to-all(f32[8,128,2048]{2,0,1:T(8,128)S(1)} %copy.8), channel_id=1, replica_groups=mesh['shard'=16,'model'=2] {'shard'}, dimensions={1} | all-to-all | bytes 16777216 | tf_op jit(solution)/shard_map/all_to_all | solution.py:27
  581.9 1.8 broadcast_multiply_fusion
  583.8 9.7 %copy.9 = f32[16,8,8,2048]{3,2,1,0:T(8,128)} copy(f32[16,8,8,2048]{3,1,2,0:T(8,128)S(1)} %bitcast.40) | data formatting | bytes 16777216 | tf_op jit(solution)/shard_map/mul | solution.py:28
  593.5 12.0 %bitcast_subtract_fusion = f32[128,8,2048]{2,1,0:T(8,128)} fusion(f32[16,8,8,2048]{3,2,1,0:T(8,128)} %copy.9, f32[128,8,2048]{2,1,0:T(8,128)} %param.5), kind=kLoop, calls=%fused_computation.1 | loop fusion | flops 4194304 | bytes 25165824 | tf_op jit(solution)/shard_map/sub | solution.py:28
  (10 shorter events, 0.7 us)
Async XLA Ops:
  7.2 252.5 %all-reduce.4.cloned.1.call-start = ((), (), s32[]{:S(2)}) async-start(), calls=%async_computation.2 | async-start | bytes 1048576 | tf_op jit(solution)/shard_map/psum | solution.py:18
  209.1 3.4 copy-start
  230.3 83.9 %all-reduce.6.cloned.1.call-start = ((), (), s32[]{:S(2)}) async-start(), calls=%async_computation.3 | async-start | bytes 1048576 | tf_op jit(solution)/shard_map/psum | solution.py:18
  273.4 3.4 copy-start.1
  285.3 85.8 %all-reduce.8.cloned.1.call-start = ((), (), s32[]{:S(2)}) async-start(), calls=%async_computation.4 | async-start | bytes 1048576 | tf_op jit(solution)/shard_map/psum | solution.py:18
  330.3 3.4 copy-start.2
Sparse Core Ops, SparseCore 0:
  230.4 29.1 all-reduce.3
  285.4 28.6 all-reduce.5
  342.4 28.6 all-reduce.7
where the time goes:
time: 618 us; the launch traced here: 612 us
  blocking collectives  383 us (62%)
  waiting for transfers between devices  86.4 us (14%)
  matrix products  76.9 us (12%)
  other arithmetic  26.6 us (4%)
  local copies, waits for them, and re-layouts  24.7 us (4%)
  between operations  14 us (2%)
    all_to_all x1, blocking collectives, body(): lax.all_to_all(new_momentum, 'shard', split_axis=0, concat_axis=1, tiled=...  190 us
    all_to_all x1, blocking collectives, body(): lax.all_to_all(iterate, 'shard', split_axis=1, concat_axis=0, tiled=True)  189 us
    psum x3, waiting for transfers between devices, body(): lax.psum(jnp.einsum('mik,mjk->mij', iterate, iterate, precision=lax.Preci...  86.4 us
    dot_general x3, matrix products, body(): jnp.einsum('mij,mjk->mik', mixed, iterate, precision=lax.Precision.HIGHEST)  40.8 us
    dot_general x3, matrix products, body(): jnp.einsum('mik,mjk->mij', iterate, iterate, precision=lax.Precision.HIGH...  29.9 us
  transfers between devices with their start and end apart: 3, of which 3 were waited for; matrix products, arithmetic and copies ran while one was open for 0% of the time, Pallas kernels for 0%

commit v1 on v0

--- a/solution.py
+++ b/solution.py
@@ -9,13 +9,18 @@
 decay_rate = 0.1
 
 
+def keep_up_steps_all(matrix, comm_axis):
+    res = lax.all_gather(matrix, comm_axis)
+    return jnp.sum(res, 0)
+
+
 def body(gradients, momentum, weights):
     new_momentum = hold_rate * momentum + gradients
     moved = lax.all_to_all(new_momentum, "shard", split_axis=0, concat_axis=1, tiled=True)
     total = lax.psum(jnp.sum(moved * moved, axis=(1, 2), keepdims=True), "model")
     iterate = moved * lax.rsqrt(total + 1e-06)
     for step in range(ITERS):
-        gram = lax.psum(
+        gram = keep_up_steps_all(
             jnp.einsum("mik,mjk->mij", iterate, iterate, precision=lax.Precision.HIGHEST), "model"
         )
         mixed = -4.775 * gram + 2.0315 * jnp.einsum(

time: 618 us -> 596 us (0.964)
  waiting for transfers between devices: 86.4 us -> 64.3 us
    psum x3 -> x0, waiting for transfers between devices: 86.4 us -> none  [body(): lax.psum(jnp.einsum('mik,mjk->mij', iterate, iterate, precision=lax.Preci...]
    all_gather x0 -> x3, waiting for transfers between devices: none -> 64.2 us  [keep_up_steps_all(): res = lax.all_gather(matrix, comm_axis)]
where the time goes in v1:
time: 596 us; the launch traced here: 590 us
  blocking collectives  383 us (64%)
  matrix products  72.7 us (12%)
  waiting for transfers between devices  64.3 us (11%)
  other arithmetic  30.6 us (5%)
  local copies, waits for them, and re-layouts  24.7 us (4%)
  between operations  14 us (2%)
    all_to_all x1, blocking collectives, body(): lax.all_to_all(new_momentum, 'shard', split_axis=0, concat_axis=1, tiled=...  190 us
    all_to_all x1, blocking collectives, body(): lax.all_to_all(iterate, 'shard', split_axis=1, concat_axis=0, tiled=True)  189 us
    all_gather x3, waiting for transfers between devices, keep_up_steps_all(): res = lax.all_gather(matrix, comm_axis)  64.2 us
    dot_general x3, matrix products, body(): jnp.einsum('mij,mjk->mik', mixed, iterate, precision=lax.Precision.HIGHEST)  40.8 us
    dot_general x3, matrix products, body(): jnp.einsum('mik,mjk->mij', iterate, iterate, precision=lax.Precision.HIGH...  30 us
    add x1, other arithmetic, body(): new_momentum = hold_rate * momentum + gradients  12 us
    sub x1, other arithmetic, body(): new_weights = (1.0 - learn_rate * decay_rate) * weights - learn_rate * back  12 us
  transfers between devices with their start and end apart: 3, of which 3 were waited for; matrix products, arithmetic and copies ran while one was open for 0% of the time, Pallas kernels for 0%

profile of v1, /device:TPU:1, one launch (start us, length us, event | category | flops | bytes accessed | tf_op | source)
XLA Modules:
  0.0 589.9 jit_solution(12277200981906233546)
XLA Ops:
  7.2 12.0 %multiply_add_fusion.3 = f32[128,8,2048]{2,1,0:T(8,128)} fusion(f32[128,8,2048]{2,1,0:T(8,128)} %param.3, f32[128,8,2048]{2,1,0:T(8,128)} %param.4), kind=kLoop, calls=%fused_computation.7 | loop fusion | flops 4194304 | bytes 25165824 | tf_op jit(solution)/shard_map/add | solution.py:18
  19.2 189.9 %all_to_all.27 = f32[128,8,2048]{2,1,0:T(8,128)S(1)} all-to-all(f32[128,8,2048]{2,1,0:T(8,128)} %multiply_add_fusion.3), channel_id=1, replica_groups=mesh['shard'=16,'model'=2] {'shard'}, dimensions={0} | all-to-all | bytes 16777216 | tf_op jit(solution)/shard_map/all_to_all | solution.py:19
  209.1 3.4 copy-done
  212.5 0.8 fusion
  213.3 4.1 psum.7
  217.3 12.9 %fusion.2 = f32[8,128,128]{2,1,0:T(8,128)} fusion(f32[16,8,8,2048]{3,2,1,0:T(8,128)} %bitcast.41, f32[8]{0:T(128)S(1)} %rsqrt_bitcast_fusion), kind=kOutput, calls=%fused_computation.9 | convolution fusion | flops 3223322624 | bytes 8912928 | tf_op jit(solution)/shard_map/mik,mjk->mij/dot_general | solution.py:24
  230.8 21.4 %all-gather.7.cloned.1.call-done = f32[16,128,128]{2,1,0:T(8,128)} async-done(((f32[8,128,128]{2,1,0:T(8,128)}), f32[16,128,128]{2,1,0:T(8,128)}) %all-gather.7.cloned.1.call-update) | async-done | bytes 1048592 | tf_op jit(solution)/shard_map/all_gather | solution.py:13
  252.3 1.3 reduce_sum.37
  254.3 11.7 %multiply_add_fusion.2 = f32[8,128,2048]{2,1,0:T(8,128)S(1)} fusion(f32[16,8,8,2048]{3,2,1,0:T(8,128)} %bitcast.42, f32[8,128,128]{2,1,0:T(8,128)S(1)} %fusion.7, f32[8]{0:T(128)S(1)} %rsqrt_bitcast_fusion), kind=kOutput, calls=%fused_computation.6 | convolution fusion | flops 3229614080 | bytes 17301536 | tf_op jit(solution)/shard_map/mij,mjk->mik/dot_general | solution.py:29
  266.0 3.4 copy-done.1
  269.3 8.5 %fusion.8 = f32[8,128,128]{2,1,0:T(8,128)} fusion(f32[8,128,2048]{2,1,0:T(8,128)S(1)} %multiply_add_fusion.2), kind=kOutput, calls=%fused_computation.20 | convolution fusion | flops 3221225472 | bytes 8912896 | tf_op jit(solution)/shard_map/mik,mjk->mij/dot_general | solution.py:24
  278.0 21.4 %all-gather.9.cloned.1.call-done = f32[16,128,128]{2,1,0:T(8,128)} async-done(((f32[8,128,128]{2,1,0:T(8,128)}), f32[16,128,128]{2,1,0:T(8,128)}) %all-gather.9.cloned.1.call-update) | async-done | bytes 1048592 | tf_op jit(solution)/shard_map/all_gather | solution.py:13
  299.3 1.3 reduce_sum.38
  301.3 14.1 %multiply_add_fusion.1 = f32[8,128,2048]{2,1,0:T(8,128)S(1)} fusion(f32[8,128,2048]{2,1,0:T(8,128)} %copy-done.1, f32[8,128,128]{2,1,0:T(8,128)S(1)} %fusion.6), kind=kOutput, calls=%fused_computation.5 | convolution fusion | flops 3225419776 | bytes 17301504 | tf_op jit(solution)/shard_map/mij,mjk->mik/dot_general | solution.py:29
  315.5 3.4 copy-done.2
  318.9 8.5 %fusion.9 = f32[8,128,128]{2,1,0:T(8,128)} fusion(f32[8,128,2048]{2,1,0:T(8,128)S(1)} %multiply_add_fusion.1), kind=kOutput, calls=%fused_computation.21 | convolution fusion | flops 3221225472 | bytes 8912896 | tf_op jit(solution)/shard_map/mik,mjk->mij/dot_general | solution.py:24
  327.4 21.4 %all-gather.11.cloned.1.call-done = f32[16,128,128]{2,1,0:T(8,128)} async-done(((f32[8,128,128]{2,1,0:T(8,128)}), f32[16,128,128]{2,1,0:T(8,128)}) %all-gather.11.cloned.1.call-update) | async-done | bytes 1048592 | tf_op jit(solution)/shard_map/all_gather | solution.py:13
  348.9 1.3 reduce_sum.39
  350.9 15.0 %multiply_add_fusion = f32[8,128,2048]{2,1,0:T(8,128)S(1)} fusion(f32[8,128,2048]{2,1,0:T(8,128)} %copy-done.2, f32[8,128,128]{2,1,0:T(8,128)S(1)} %fusion.5), kind=kOutput, calls=%fused_computation.4 | convolution fusion | flops 3225419776 | bytes 17301504 | tf_op jit(solution)/shard_map/mij,mjk->mik/dot_general | solution.py:29
  365.9 4.9 copy.8
  370.8 188.9 %all_to_all.28 = f32[8,128,2048]{2,0,1:T(8,128)S(1)} all-to-all(f32[8,128,2048]{2,0,1:T(8,128)S(1)} %copy.8), channel_id=1, replica_groups=mesh['shard'=16,'model'=2] {'shard'}, dimensions={1} | all-to-all | bytes 16777216 | tf_op jit(solution)/shard_map/all_to_all | solution.py:32
  559.6 1.8 broadcast_multiply_fusion
  561.5 9.7 %copy.9 = f32[16,8,8,2048]{3,2,1,0:T(8,128)} copy(f32[16,8,8,2048]{3,1,2,0:T(8,128)S(1)} %bitcast.43) | data formatting | bytes 16777216 | tf_op jit(solution)/shard_map/mul | solution.py:33
  571.2 12.0 %bitcast_subtract_fusion = f32[128,8,2048]{2,1,0:T(8,128)} fusion(f32[16,8,8,2048]{3,2,1,0:T(8,128)} %copy.9, f32[128,8,2048]{2,1,0:T(8,128)} %param.5), kind=kLoop, calls=%fused_computation.1 | loop fusion | flops 4194304 | bytes 25165824 | tf_op jit(solution)/shard_map/sub | solution.py:33
  (13 shorter events, 2.7 us)
Async XLA Ops:
  7.2 245.1 %all-gather.7.cloned.1.call-start = ((), (), s32[]{:S(2)}) async-start(), calls=%async_computation.2 | async-start | bytes 1572864 | tf_op jit(solution)/shard_map/all_gather | solution.py:13
  209.1 3.4 copy-start
  230.3 69.1 %all-gather.9.cloned.1.call-start = ((), (), s32[]{:S(2)}) async-start(), calls=%async_computation.3 | async-start | bytes 1572864 | tf_op jit(solution)/shard_map/all_gather | solution.py:13
  265.9 3.4 copy-start.1
  277.9 71.0 %all-gather.11.cloned.1.call-start = ((), (), s32[]{:S(2)}) async-start(), calls=%async_computation.4 | async-start | bytes 1572864 | tf_op jit(solution)/shard_map/all_gather | solution.py:13
  315.5 3.4 copy-start.2
Sparse Core Ops, SparseCore 0:
  230.4 21.8 all-gather.6
  278.0 21.2 all-gather.8
  327.5 21.2 all-gather.10
